TPU v7x, 32 devices: a whole 2x2x4 slice. The times are simulated.
32 devices in a mesh: dp: 8 (over y, x, core), mp: 4 (over z).
Axes of the slice: x: 2, y: 2, z: 4, core: 2. Of those that a mesh axis runs over, the one named last changes fastest.
Arguments:
- tokens: bfloat16 [16384, 1024], P(('dp', 'mp')), may hold values from -6 to 6
- norm_gain: float32 [2, 1024], replicated, may hold values from 0.1 to 1.9
- qkv_weight: bfloat16 [3, 1024, 1024], P(None, 'dp', 'mp')
- out_weight: bfloat16 [1024, 1024], P('mp', 'dp'), may hold values from -0.1875 to 0.1875
- variate_bias: float32 [2, 16], replicated, may hold values from -6 to 6
- ffn_weight: bfloat16 [2, 1024, 2816], P(None, 'dp', 'mp'), may hold values from -0.1875 to 0.1875
- down_weight: bfloat16 [2816, 1024], P('mp', 'dp'), may hold values from -0.109375 to 0.109375
- sample_ids: int32 [16384], P(('dp', 'mp')), may hold values from 0 to 127, as said below
- variate_ids: int32 [16384], P(('dp', 'mp')), may hold values from 0 to 15, as said below
- time_ids: int32 [16384], P(('dp', 'mp')), may hold values from 0 to 31, as said below
Outputs:
- encoded: bfloat16 [16384, 1024], P(('dp', 'mp'))
Inputs may be any that keep to these rules, and one draw needn't show every extreme that they name: `sample_ids`: within each packed sequence of 512 tokens the series numbers start at 0 and never fall; a series with v variates (1 to 16) and p patches (4 to 32) holds v * p consecutive tokens, the last series of a sequence may be cut short; some packed sequence holds 128 series of one variate and four patches each. `variate_ids`: A token's offset within its series divided by that series' patch count p. `time_ids`: A token's offset within its series modulo that series' patch count p.
All inputs are finite; a program needn't handle non-finite values.
Results may differ from a plain program's by a relative error of at most 0.017.
Values may be sent and summed in bfloat16 or wider, within the bound.
A program may use at most 128 MiB of HBM per device.

v0:
```python
import functools
import math

import jax
import jax.numpy as jnp
from jax import lax
from jax.experimental import pallas as pl
from jax.experimental.pallas import tpu as pltpu
from jax.sharding import PartitionSpec as P

HEAD_DIM = 64
L = 512


def rms_norm(values, gain):
    wide = values.astype(jnp.float32)
    square = jnp.mean(wide * wide, axis=-1, keepdims=True)
    return (wide * lax.rsqrt(square + 1e-05) * gain[None, :]).astype(jnp.bfloat16)


def rotate(values, times):
    half = values.shape[-1] // 2
    freq = 10000.0 ** (-jnp.arange(half, dtype=jnp.float32) / half)
    angle = times.astype(jnp.float32)[:, None] * freq[None, :]
    cosine = jnp.cos(angle)[:, None, :]
    sine = jnp.sin(angle)[:, None, :]
    first = values[..., :half]
    second = values[..., half:]
    return jnp.concatenate(
        [first * cosine - second * sine, first * sine + second * cosine], axis=-1
    )


def rotated(raw, times):
    row_total, local_width = raw.shape
    turned = rotate(raw.reshape(row_total, local_width // HEAD_DIM, HEAD_DIM), times)
    return turned.reshape(row_total, local_width).astype(jnp.bfloat16)


def attend(queries, keys_rot, values, samples, variates, bias):
    row_total, local_width = queries.shape
    heads_here = local_width // HEAD_DIM
    count = row_total // L

    def one_sequence(args):
        qs, ks, vs, sample_row, variate_row = args
        scores = jnp.einsum(
            "qhd,khd->hqk", qs, ks, preferred_element_type=jnp.float32
        ) * HEAD_DIM ** (-0.5)
        same = variate_row[:, None] == variate_row[None, :]
        scores = scores + jnp.where(same[None], bias[0][:, None, None], bias[1][:, None, None])
        scores = jnp.where((sample_row[:, None] == sample_row[None, :])[None], scores, -1e30)
        top = jnp.max(scores, axis=2, keepdims=True)
        expo = jnp.exp(scores - top)
        weights = (expo / jnp.sum(expo, axis=2, keepdims=True)).astype(jnp.bfloat16)
        return jnp.einsum("hqk,khd->qhd", weights, vs, preferred_element_type=jnp.float32).astype(
            jnp.bfloat16
        )

    shape = (count, L, heads_here, HEAD_DIM)
    result = lax.map(
        one_sequence,
        (
            queries.reshape(shape),
            keys_rot.reshape(shape),
            values.reshape(shape),
            samples.reshape(count, L),
            variates.reshape(count, L),
        ),
    )
    return result.reshape(row_total, local_width)


def local(
    tokens,
    norm_gain,
    qkv_weight,
    out_weight,
    variate_bias,
    ffn_weight,
    down_weight,
    sample_ids,
    variate_ids,
    time_ids,
):
    first_normed = rms_norm(tokens, norm_gain[0])
    wide_columns = lax.all_gather(qkv_weight, "mp", axis=2, tiled=True)
    columns = first_normed
    projected = jnp.einsum(
        "rc,jcd->jrd",
        columns,
        lax.all_gather(wide_columns, "dp", axis=1, tiled=True),
        preferred_element_type=jnp.float32,
    )
    queries = rotated(projected[0], time_ids)
    keys_rot = rotated(projected[1], time_ids)
    values = projected[2].astype(jnp.bfloat16)
    back_rows = attend(queries, keys_rot, values, sample_ids, variate_ids, variate_bias)
    out_rows = lax.all_gather(out_weight, "mp", axis=0, tiled=True)
    mixed = jnp.dot(
        back_rows,
        lax.all_gather(out_rows, "dp", axis=1, tiled=True),
        preferred_element_type=jnp.float32,
    )
    residual = (tokens.astype(jnp.float32) + mixed).astype(jnp.bfloat16)
    second_normed = rms_norm(residual, norm_gain[1])
    ffn_columns = lax.all_gather(ffn_weight, "mp", axis=2, tiled=True)
    columns = second_normed
    gate_up = jnp.einsum(
        "rc,jcf->jrf",
        columns,
        lax.all_gather(ffn_columns, "dp", axis=1, tiled=True),
        preferred_element_type=jnp.float32,
    )
    hidden = (jax.nn.silu(gate_up[0]) * gate_up[1]).astype(jnp.bfloat16)
    down_full = lax.all_gather(down_weight, "mp", axis=0, tiled=True)
    feed = jnp.dot(
        hidden,
        lax.all_gather(down_full, "dp", axis=1, tiled=True),
        preferred_element_type=jnp.float32,
    )
    return (residual.astype(jnp.float32) + feed).astype(jnp.bfloat16)

MESH = pl.DeviceIdType.MESH
PIECES = 4
ROWS = 256
WIDE = 2 * HEAD_DIM
STAGES = 7
ARRAY_TURNS = 1.5
LATE_TURNS = 1.2


def event_order(arrays):
    due = []
    for which in range(arrays):
        for stage in range(STAGES):
            for late in range(2):
                due.append((which * ARRAY_TURNS + stage + late * LATE_TURNS, which, stage, late))
    return [item[1:] for item in sorted(due)]


def layer_kernel(
    ring,
    bias_ref, tokens_ref, gain_ref, ids_ref, qkv_in, out_in, ffn_in, down_in,
    final_ref,
    qkv_buf, out_buf, gate_buf, up_buf, down_buf,
    normed, queries, keys, values, attended, residual, gates, hidden, cosine, sine, columns,
    send_sem, recv_sem, local_sem,
):
    bufs = (qkv_buf, out_buf, gate_buf, up_buf, down_buf)
    dp = lax.axis_index("dp")
    z = lax.axis_index("mp")
    core = lax.rem(dp, 2)
    x = lax.rem(dp // 2, 2)
    y = dp // 4
    up_z = lax.rem(z + 1, ring)
    down_z = lax.rem(z + ring - 1, ring)
    whole = slice(None)
    to_x = {"dp": (y * 2 + 1 - x) * 2 + core, "mp": z}
    to_y = {"dp": ((1 - y) * 2 + x) * 2 + core, "mp": z}
    to_core = {"dp": (y * 2 + x) * 2 + 1 - core, "mp": z}
    to_up = {"dp": dp, "mp": up_z}
    to_down = {"dp": dp, "mp": down_z}
    steps = ring - 1
    first_pair, second_pair, across = 2 * steps, 2 * steps + 1, 2 * steps + 2
    hops = 2 * steps + 3

    def x_leads(which, piece):
        return (which + piece) % 2 == 0

    def z_leads(piece):
        return piece < PIECES - 1

    def target(which, piece, hop):
        if hop < steps:
            return to_up
        if hop < 2 * steps:
            return to_down
        if hop == across:
            return to_core
        return to_x if (hop == first_pair) == x_leads(which, piece) else to_y

    def region(which, piece, hop):
        pair = (y, whole) if x_leads(which, piece) else (whole, x)
        if hop == across:
            return (whole, whole, core, whole)
        if hop == first_pair:
            return (y, x, core, whole if z_leads(piece) else z)
        if hop == second_pair:
            return pair + (core, whole if z_leads(piece) else z)
        block = z - hop if hop < steps else z + (hop - steps)
        return ((y, x) if z_leads(piece) else (whole, whole)) + (core, block)

    def sends_now(hop):
        if hop < steps:
            return jnp.logical_and(z >= hop, z < ring - 1)
        return jnp.logical_and(z + (hop - steps) < ring, z > 0)

    def lands_now(hop):
        if hop < steps:
            return z >= hop + 1
        return z + (hop - steps) + 1 < ring

    def copy(which, piece, hop, fixed=False):
        at = region(which, piece, hop)
        if fixed and hop < 2 * steps:
            at = at[:3] + (z,)
        part = bufs[which].at[at + (whole, piece)]
        slot = (which * PIECES + piece) * hops + hop
        return pltpu.make_async_remote_copy(
            src_ref=part, dst_ref=part, send_sem=send_sem.at[slot], recv_sem=recv_sem.at[slot],
            device_id=target(which, piece, hop), device_id_type=MESH,
        )

    def guarded(hop, condition, action):
        if hop < 2 * steps:
            pl.when(condition(hop))(action)
        else:
            action()

    def send(which, piece, hop):
        guarded(hop, sends_now, lambda: copy(which, piece, hop).start())

    def land(which, piece, hop):
        guarded(hop, lands_now, lambda: copy(which, piece, hop, True).wait_recv())

    def sent(which, piece, hop):
        guarded(hop, sends_now, lambda: copy(which, piece, hop, True).wait_send())

    def own(which):
        source = (qkv_in, out_in, ffn_in.at[pl.ds(0, 1)], ffn_in.at[pl.ds(1, 1)], down_in)[which]
        return pltpu.make_async_copy(source, bufs[which].at[y, x, core, z], local_sem.at[which])

    line = [((), (0, steps))]
    for step in range(1, steps):
        line.append(((step - 1, steps + step - 1), (step, steps + step)))
    line_end = (steps - 1, 2 * steps - 1)
    z_first = line + [
        (line_end, (first_pair,)), ((first_pair,), (second_pair,)), ((second_pair,), (across,)),
        ((across,), ()),
    ]
    z_last = [((), (first_pair,)), ((first_pair,), (second_pair,)), ((second_pair,), line[0][1])]
    z_last += line[1:] + [(line_end, (across,)), ((across,), ())]

    def event(which, stage, late):
        for piece in range(PIECES):
            if z_leads(piece) == bool(late):
                continue
            waits, sends = (z_first if z_leads(piece) else z_last)[stage]
            for hop in waits:
                land(which, piece, hop)
            for hop in sends:
                send(which, piece, hop)

    order = event_order(len(bufs))
    cursor = [0]

    def take(count):
        picked = order[cursor[0]:cursor[0] + count]
        cursor[0] += len(picked)
        return picked

    def until(which):
        ends = [order.index((which, STAGES - 1, late)) for late in range(2)]
        return take(max(ends) + 1 - cursor[0])

    def at_steps(total, picked):
        plan = [[] for _ in range(total)]
        for place, item in enumerate(picked):
            plan[place * total // len(picked)].append(item)

        def run(step):
            for place, items in enumerate(plan):
                if items:
                    @pl.when(step == place)
                    def _():
                        for item in items:
                            event(*item)
        return run

    for which in range(len(bufs)):
        own(which).start()
    barrier = pltpu.get_barrier_semaphore()
    for peer in (to_x, to_y, to_core, to_up, to_down):
        pl.semaphore_signal(barrier, inc=1, device_id=peer, device_id_type=MESH)
    pl.semaphore_wait(barrier, 5)
    for which in range(len(bufs)):
        own(which).wait()

    first_wave = until(0)
    cut = min(3, len(first_wave))
    for item in first_wave[:cut]:
        event(*item)

    total_rows, width = tokens_ref.shape
    blocks = total_rows // ROWS

    def norm_rows(source, gain_row):
        gain = gain_ref[gain_row:gain_row + 1, :]

        def body(step, carry):
            rows = pl.ds(pl.multiple_of(step * 128, 128), 128)
            wide = source[rows, :].astype(jnp.float32)
            square = jnp.mean(wide * wide, axis=-1, keepdims=True)
            normed[rows, :] = (wide * lax.rsqrt(square + 1e-05) * gain).astype(jnp.bfloat16)
            return carry
        lax.fori_loop(0, total_rows // 128, body, 0)

    norm_rows(tokens_ref, 0)
    ids = ids_ref[...].astype(jnp.float32)
    times = jnp.broadcast_to(ids[2:3, :], (WIDE, total_rows)).T
    columns[0] = jnp.broadcast_to(ids[0:1, :], (WIDE, total_rows)).T
    columns[1] = jnp.broadcast_to(ids[1:2, :], (WIDE, total_rows)).T
    half = HEAD_DIM // 2
    lane = lax.broadcasted_iota(jnp.int32, (1, WIDE), 1)
    slot_in_half = lax.rem(lane, half).astype(jnp.float32)
    freq = jnp.exp(slot_in_half * (-math.log(10000.0) / half))
    front = lax.rem(lane, HEAD_DIM) < half
    angle = times * freq
    cosine[...] = jnp.cos(angle)
    sine[...] = jnp.where(front, -1.0, 1.0) * jnp.sin(angle)

    for item in first_wave[cut:]:
        event(*item)

    def rotated_wide(raw):
        swapped = jnp.where(front, pltpu.roll(raw, WIDE - half, 1), pltpu.roll(raw, half, 1))
        return raw * cosine[...] + swapped * sine[...]

    later = until(2)
    early_count = min(len(later), 3)
    project_events = at_steps(ring, later[:early_count])
    attend_steps = (width // WIDE) * blocks
    attend_events = at_steps(attend_steps, later[early_count:])

    def project(step, carry):
        def product(kind):
            shape = (width, qkv_buf.shape[-1])
            weight = qkv_buf[:, :, :, step, kind].reshape(shape)
            return jnp.dot(normed[...], weight, preferred_element_type=jnp.float32)
        groups = qkv_buf.shape[-1] // WIDE
        for kind, held in enumerate((queries, keys, values)):
            raw = product(kind)
            for group in range(groups):
                part = raw[:, group * WIDE:(group + 1) * WIDE]
                if kind < 2:
                    part = rotated_wide(part)
                part = part.astype(jnp.bfloat16)
                if kind == 0:
                    part = part * jnp.bfloat16(HEAD_DIM ** -0.5)
                held[step * groups + group] = part
        project_events(step)
        return carry
    lax.fori_loop(0, ring, project, 0)

    left = lane < HEAD_DIM

    def attend_step(step, carry):
        pair = step // blocks
        block = lax.rem(step, blocks)
        rows = pl.ds(pl.multiple_of(block * ROWS, ROWS), ROWS)
        base = pl.multiple_of((block * ROWS) // L * L, L)
        span = pl.ds(base, L)
        same_series = columns[0, rows, 0:1] == ids_ref[0:1, span].astype(jnp.float32)
        same_variate = columns[1, rows, 0:1] == ids_ref[1:2, span].astype(jnp.float32)
        both = queries[pair, rows, :]
        key_rows = keys[pair, span, :]
        value_rows = values[pair, span, :]
        results = []
        for side in range(2):
            head = pair * 2 + side
            chosen = left if side == 0 else jnp.logical_not(left)
            mine = both * chosen.astype(jnp.bfloat16)
            scores = lax.dot_general(
                mine, key_rows, (((1,), (1,)), ((), ())), preferred_element_type=jnp.float32
            )
            scores = scores + jnp.where(same_variate, bias_ref[0, head], bias_ref[1, head])
            scores = jnp.where(same_series, scores, -1e30)
            top = jnp.max(scores, axis=1, keepdims=True)
            expo = jnp.exp(scores - top)
            total = jnp.sum(expo, axis=1, keepdims=True)
            mixed = jnp.dot(
                expo.astype(jnp.bfloat16), value_rows, preferred_element_type=jnp.float32
            )
            results.append(mixed / total)
        lanes = pl.ds(pl.multiple_of(pair * WIDE, WIDE), WIDE)
        attended[rows, lanes] = jnp.where(left, results[0], results[1]).astype(jnp.bfloat16)
        attend_events(step)
        return carry
    lax.fori_loop(0, attend_steps, attend_step, 0)

    def block_pair(buf, side_y, side_x, index):
        return jnp.concatenate(
            [buf[side_y, side_x, half_core, index].reshape(-1, buf.shape[-1]) for half_core in range(2)],
            axis=1,
        )

    slab = 2 * out_buf.shape[-1]

    def out_step(step, carry):
        lanes = pl.ds(pl.multiple_of(step * slab, slab), slab)
        weight = block_pair(out_buf, step // 2, lax.rem(step, 2), whole)
        mixed = jnp.dot(attended[...], weight, preferred_element_type=jnp.float32)
        residual[:, lanes] = (tokens_ref[:, lanes].astype(jnp.float32) + mixed).astype(jnp.bfloat16)
        return carry
    lax.fori_loop(0, 4, out_step, 0)
    norm_rows(residual, 1)

    gate_events = at_steps(ring, until(3))

    def gate_step(step, carry):
        weight = gate_buf[:, :, :, step].reshape(width, gate_buf.shape[-1])
        gates[step] = jnp.dot(normed[...], weight, preferred_element_type=jnp.float32)
        gate_events(step)
        return carry
    lax.fori_loop(0, ring, gate_step, 0)

    up_events = at_steps(ring, until(4))

    def up_step(step, carry):
        weight = up_buf[:, :, :, step].reshape(width, up_buf.shape[-1])
        up = jnp.dot(normed[...], weight, preferred_element_type=jnp.float32)
        gate = gates[step]
        hidden[step] = (gate / (1.0 + jnp.exp(-gate)) * up).astype(jnp.bfloat16)
        up_events(step)
        return carry
    lax.fori_loop(0, ring, up_step, 0)

    def down_step(step, carry):
        lanes = pl.ds(pl.multiple_of(step * slab, slab), slab)
        total = residual[:, lanes].astype(jnp.float32)
        for index in range(ring):
            weight = block_pair(down_buf, step // 2, lax.rem(step, 2), index)
            total = total + jnp.dot(hidden[index], weight, preferred_element_type=jnp.float32)
        final_ref[:, lanes] = total.astype(jnp.bfloat16)
        return carry
    lax.fori_loop(0, 4, down_step, 0)

    for which in range(len(bufs)):
        for piece in range(PIECES):
            for hop in range(hops):
                sent(which, piece, hop)


def fused(
    ring, tokens, norm_gain, qkv_weight, out_weight, variate_bias, ffn_weight, down_weight,
    sample_ids, variate_ids, time_ids,
):
    rows, width = tokens.shape
    ids = jnp.stack([sample_ids, variate_ids, time_ids])
    qkv = qkv_weight.reshape(qkv_weight.shape[0], PIECES, -1, qkv_weight.shape[2])
    out = out_weight.reshape(1, PIECES, -1, out_weight.shape[1])
    ffn = ffn_weight.reshape(2, PIECES, -1, ffn_weight.shape[2])
    down = down_weight.reshape(1, PIECES, -1, down_weight.shape[1])
    shapes = (qkv.shape, out.shape, (1,) + ffn.shape[1:], (1,) + ffn.shape[1:], down.shape)
    buffers = [pltpu.VMEM((2, 2, 2, ring) + shape, jnp.bfloat16) for shape in shapes]
    pairs = width // WIDE
    per_pair = pltpu.VMEM((pairs, rows, WIDE), jnp.bfloat16)
    flat = pltpu.VMEM((rows, width), jnp.bfloat16)
    vmem = pl.BlockSpec(memory_space=pltpu.VMEM)
    anywhere = pl.BlockSpec(memory_space=pl.ANY)
    copies = len(shapes) * PIECES * (2 * ring + 1)
    return pl.pallas_call(
        functools.partial(layer_kernel, ring),
        out_shape=jax.ShapeDtypeStruct((rows, width), jnp.bfloat16),
        in_specs=[pl.BlockSpec(memory_space=pltpu.SMEM), vmem, vmem, vmem] + [anywhere] * 4,
        out_specs=vmem,
        scratch_shapes=buffers + [
            flat, per_pair, per_pair, per_pair, flat, flat,
            pltpu.VMEM((ring, rows, ffn.shape[-1]), jnp.float32),
            pltpu.VMEM((ring, rows, ffn.shape[-1]), jnp.bfloat16),
            pltpu.VMEM((rows, WIDE), jnp.float32),
            pltpu.VMEM((rows, WIDE), jnp.float32),
            pltpu.VMEM((2, rows, WIDE), jnp.float32),
            pltpu.SemaphoreType.DMA((copies,)),
            pltpu.SemaphoreType.DMA((copies,)),
            pltpu.SemaphoreType.DMA((len(shapes),)),
        ],
        compiler_params=pltpu.CompilerParams(
            collective_id=0, has_side_effects=True, vmem_limit_bytes=60 * 1024 * 1024
        ),
    )(variate_bias, tokens, norm_gain, ids, qkv, out, ffn, down)


def solution(mesh):
    ring = mesh.shape["mp"]
    body = functools.partial(fused, ring) if (mesh.shape["dp"], ring) == (2 ** 3, 2 ** 2) else local
    return jax.shard_map(
        body,
        mesh=mesh,
        in_specs=(
            P(("dp", "mp"), None),
            P(),
            P(None, "dp", "mp"),
            P("mp", "dp"),
            P(),
            P(None, "dp", "mp"),
            P("mp", "dp"),
            P(("dp", "mp")),
            P(("dp", "mp")),
            P(("dp", "mp")),
        ),
        out_specs=P(("dp", "mp"), None),
        check_vma=False,
    )
```

profile of v0, /device:TPU:1, one launch (start us, length us, event | category | flops | bytes accessed | tf_op | source)
XLA Modules:
  0.0 134.4 jit_solution(7722464569115222224)
XLA Ops:
  0.0 0.0 copy-start.2
  0.0 0.0 copy-start.1
  0.0 0.0 copy-start
  0.0 0.7 copy-done.2
  0.7 0.0 copy-done.1
  0.7 0.0 copy-done
  0.7 0.6 pad_add_fusion.ids_ref
  1.3 1.9 %copy.11 = bf16[2,128,704]{2,1,0:T(8,128)(2,1)} copy(bf16[2,128,704]{1,2,0:T(8,128)(2,1)} %param.15) | data formatting | bytes 720896 | tf_op args[5]
  3.2 128.9 %shard_map.100 = bf16[512,1024]{1,0:T(8,128)(2,1)} custom-call(f32[2,16]{1,0:T(2,128)} %bias_ref.1, bf16[512,1024]{1,0:T(8,128)(2,1)} %tokens_ref.1, f32[2,1024]{1,0:T(2,128)} %gain_ref.1, s32[3,512]{1,0:T(4,128)} %pad_add_fusion.ids_ref, bf16[3,4,32,256]{3,2,1,0:T(8,128)(2,1)} %bitcast.8, bf16[1,4,64,128]{3,2,1,0:T(8,128)(2,1)} %bitcast.10, ...), custom_call_target="tpu_custom_call" | custom-call | tf_op jit(solution)/shard_map/pallas_call | solution.py:463
  132.1 2.3 %copy.13 = bf16[512,1024]{1,0:T(8,128)(2,1)} copy(bf16[512,1024]{1,0:T(8,128)(2,1)} %shard_map.100) | data formatting | bytes 2097152
Async XLA Ops:
  0.0 0.7 copy-start.2
  0.0 0.7 copy-start.1
  0.0 0.7 copy-start
where the time goes:
time: 135 us; the launch traced here: 134 us
  Pallas kernels  129 us (96%)
  local copies, waits for them, and re-layouts  4.87 us (4%)
    pallas_call x1, Pallas kernels, fused(): pl.pallas_call(functools.partial(layer_kernel, ring), out_shape=jax.Shape...  129 us
    unnamed x8, local copies, waits for them, and re-layouts  4.87 us

commit v1 on v0

v1 whole, which is shorter than its diff:
```python
import functools
import math

import jax
import jax.numpy as jnp
from jax import lax
from jax.experimental import pallas as pl
from jax.experimental.pallas import tpu as pltpu
from jax.sharding import PartitionSpec as P

HEAD_DIM = 64
L = 512


def rms_norm(values, gain):
    wide = values.astype(jnp.float32)
    square = jnp.mean(wide * wide, axis=-1, keepdims=True)
    return (wide * lax.rsqrt(square + 1e-05) * gain[None, :]).astype(jnp.bfloat16)


def rotate(values, times):
    half = values.shape[-1] // 2
    freq = 10000.0 ** (-jnp.arange(half, dtype=jnp.float32) / half)
    angle = times.astype(jnp.float32)[:, None] * freq[None, :]
    cosine = jnp.cos(angle)[:, None, :]
    sine = jnp.sin(angle)[:, None, :]
    first = values[..., :half]
    second = values[..., half:]
    return jnp.concatenate(
        [first * cosine - second * sine, first * sine + second * cosine], axis=-1
    )


def rotated(raw, times):
    row_total, local_width = raw.shape
    turned = rotate(raw.reshape(row_total, local_width // HEAD_DIM, HEAD_DIM), times)
    return turned.reshape(row_total, local_width).astype(jnp.bfloat16)


def attend(queries, keys_rot, values, samples, variates, bias):
    row_total, local_width = queries.shape
    heads_here = local_width // HEAD_DIM
    count = row_total // L

    def one_sequence(args):
        qs, ks, vs, sample_row, variate_row = args
        scores = jnp.einsum(
            "qhd,khd->hqk", qs, ks, preferred_element_type=jnp.float32
        ) * HEAD_DIM ** (-0.5)
        same = variate_row[:, None] == variate_row[None, :]
        scores = scores + jnp.where(same[None], bias[0][:, None, None], bias[1][:, None, None])
        scores = jnp.where((sample_row[:, None] == sample_row[None, :])[None], scores, -1e30)
        top = jnp.max(scores, axis=2, keepdims=True)
        expo = jnp.exp(scores - top)
        weights = (expo / jnp.sum(expo, axis=2, keepdims=True)).astype(jnp.bfloat16)
        return jnp.einsum("hqk,khd->qhd", weights, vs, preferred_element_type=jnp.float32).astype(
            jnp.bfloat16
        )

    shape = (count, L, heads_here, HEAD_DIM)
    result = lax.map(
        one_sequence,
        (
            queries.reshape(shape),
            keys_rot.reshape(shape),
            values.reshape(shape),
            samples.reshape(count, L),
            variates.reshape(count, L),
        ),
    )
    return result.reshape(row_total, local_width)


def local(
    tokens,
    norm_gain,
    qkv_weight,
    out_weight,
    variate_bias,
    ffn_weight,
    down_weight,
    sample_ids,
    variate_ids,
    time_ids,
):
    first_normed = rms_norm(tokens, norm_gain[0])
    wide_columns = lax.all_gather(qkv_weight, "mp", axis=2, tiled=True)
    columns = first_normed
    projected = jnp.einsum(
        "rc,jcd->jrd",
        columns,
        lax.all_gather(wide_columns, "dp", axis=1, tiled=True),
        preferred_element_type=jnp.float32,
    )
    queries = rotated(projected[0], time_ids)
    keys_rot = rotated(projected[1], time_ids)
    values = projected[2].astype(jnp.bfloat16)
    back_rows = attend(queries, keys_rot, values, sample_ids, variate_ids, variate_bias)
    out_rows = lax.all_gather(out_weight, "mp", axis=0, tiled=True)
    mixed = jnp.dot(
        back_rows,
        lax.all_gather(out_rows, "dp", axis=1, tiled=True),
        preferred_element_type=jnp.float32,
    )
    residual = (tokens.astype(jnp.float32) + mixed).astype(jnp.bfloat16)
    second_normed = rms_norm(residual, norm_gain[1])
    ffn_columns = lax.all_gather(ffn_weight, "mp", axis=2, tiled=True)
    columns = second_normed
    gate_up = jnp.einsum(
        "rc,jcf->jrf",
        columns,
        lax.all_gather(ffn_columns, "dp", axis=1, tiled=True),
        preferred_element_type=jnp.float32,
    )
    hidden = (jax.nn.silu(gate_up[0]) * gate_up[1]).astype(jnp.bfloat16)
    down_full = lax.all_gather(down_weight, "mp", axis=0, tiled=True)
    feed = jnp.dot(
        hidden,
        lax.all_gather(down_full, "dp", axis=1, tiled=True),
        preferred_element_type=jnp.float32,
    )
    return (residual.astype(jnp.float32) + feed).astype(jnp.bfloat16)

MESH = pl.DeviceIdType.MESH
WIDE = 2 * HEAD_DIM
ROWS = 256
LAYOUT = (2 ** 3, 2 ** 2)
HALVES = 2
FF_PARTS = 4
LOG2E = math.log2(math.e)
SLOTS = ("zp", "zoE", "zoM", "zf", "p1", "p2", "a1", "a2")
KINDS = "AAAAAAABBAAAAAAABBAA"
LEADS = "xyxyxyxxyyxyxyxyxyxy"
PLAN = (
    ((0, 0), (1, 0), (16, 0), (7, 0), (8, 0), (4, 0), (3, 0), (2, 0),),
    (),
    (),
    ((0, 1), (16, 1), (1, 1), (7, 1), (8, 1), (17, 0), (0, 2), (1, 2), (4, 1), (3, 1), (2, 1), (5, 0), (6, 0), (4, 2), (10, 0), (3, 2), (2, 2), (17, 1), (11, 0), (9, 0), (13, 0), (0, 3), (1, 3), (5, 1), (12, 0), (14, 0), (6, 1), (10, 1), (4, 3), (3, 3), (15, 0), (5, 2), (2, 3), (6, 2), (11, 1), (9, 1), (10, 2), (13, 1), (18, 0), (19, 0), (0, 4), (11, 2), (12, 1), (14, 1), (1, 4), (9, 2), (0, 5),),
    (),
    ((13, 2), (1, 5), (16, 2), (15, 1), (7, 2),),
    (),
    ((12, 2), (14, 2), (4, 4), (3, 4), (5, 3), (8, 2), (2, 4), (6, 3), (4, 5), (3, 5), (18, 1), (19, 1), (2, 5), (10, 3),),
    (),
    (),
    ((15, 2),),
    ((11, 3),),
    (),
    (),
    (),
    (),
    (),
    (),
    (),
    (),
    (),
    ((18, 2), (16, 3), (19, 2), (9, 3), (7, 3), (13, 3), (8, 3), (17, 2), (12, 3), (14, 3), (5, 4), (6, 4), (5, 5),),
    (),
    (),
    (),
    (),
    (),
    (),
    ((15, 3), (10, 4), (6, 5), (16, 4),),
    (),
    ((7, 4),),
    ((10, 5), (16, 5), (7, 5), (18, 3), (19, 3), (11, 4),),
    (),
    (),
    (),
    (),
    ((8, 4), (9, 4), (13, 4), (17, 3), (11, 5), (8, 5),),
    ((9, 5),),
    ((13, 5), (12, 4),),
    (),
    (),
    ((14, 4), (12, 5),),
    (),
    ((14, 5), (15, 4),),
    (),
    ((15, 5), (17, 4),),
    (),
    (),
    ((18, 4), (17, 5),),
    ((19, 4), (18, 5),),
    ((19, 5),),
    (),
)


def stages(kind, lead):
    other = "y" if lead == "x" else "x"
    if kind == "A":
        return [
            ((), (("zp", "z"), ("zo", "z"))),
            (("ZM",), (("zf", "z"),)),
            (("ZP", "ZF"), (("p1", lead),)),
            (("p1",), (("p2", other), ("a1", "c"))),
            (("p2",), (("a2", "c"),)),
            (("a1", "a2"), ()),
        ]
    return [
        ((), (("p1", lead),)),
        (("p1",), (("p2", other),)),
        (("p2",), (("zp", "z"), ("zo", "z"))),
        (("ZM",), (("zf", "z"),)),
        (("ZP", "ZF"), (("a2", "c"),)),
        (("a2",), ()),
    ]


def layer_kernel(
    spans,
    bias_ref, gain_ref, sample_ref, variate_ref, time_ref, tokens_in, qkv_in, out_in, ffn_in, down_in,
    final_ref,
    weights, tokens, normed, queries, keys, values, attended, residual, gate, hidden, total,
    cosine, sine, kinds, mask, result, send_sem, recv_sem, local_sem, token_sem, result_sem,
):
    dp = lax.axis_index("dp")
    z = lax.axis_index("mp")
    core = lax.rem(dp, 2)
    x = lax.rem(dp // 2, 2)
    y = dp // 4
    whole = slice(None)
    is_mid = jnp.logical_or(z == 1, z == 2)
    low = z < 2
    partner_z = z + 1 - 2 * lax.rem(z, 2)
    far_mid = jnp.where(low, 2, 1)
    far_end = jnp.where(low, 3, 0)
    far_half = pl.ds(jnp.where(low, 2, 0), 2)
    to = {
        "x": {"dp": (y * 2 + 1 - x) * 2 + core, "mp": z},
        "y": {"dp": ((1 - y) * 2 + x) * 2 + core, "mp": z},
        "c": {"dp": (y * 2 + x) * 2 + 1 - core, "mp": z},
        "zp": {"dp": dp, "mp": partner_z},
        "zo": {"dp": dp, "mp": far_mid},
        "far": {"dp": dp, "mp": far_end},
    }
    to["zf"] = to["zp"]

    def region(chunk, name):
        kind, lead = KINDS[chunk], LEADS[chunk]
        if name in ("zp", "zo"):
            head = (y, x, core, z) if kind == "A" else (whole, whole, core, z)
        elif name == "zf":
            head = (y, x, core, far_half) if kind == "A" else (whole, whole, core, far_half)
        elif name == "p1":
            head = (y, x, core, whole) if kind == "A" else (y, x, core, z)
        else:
            cut = slice(None) if kind == "A" else z
            if name == "p2":
                head = ((y, whole) if lead == "x" else (whole, x)) + (core, cut)
            elif name == "a1":
                head = ((y, whole) if lead == "x" else (whole, x)) + (core, whole)
            elif kind == "A":
                head = ((1 - y, whole) if lead == "x" else (whole, 1 - x)) + (core, whole)
            else:
                head = (whole, whole, core, whole)
        start, rows = spans[chunk]
        return head + (pl.ds(start, rows),)

    def copy(chunk, name, target, landing=None):
        part = weights.at[region(chunk, name)]
        slot = chunk * len(SLOTS)
        if name == "zo" and landing is None:
            slot = slot + jnp.where(is_mid, SLOTS.index("zoM"), SLOTS.index("zoE"))
        else:
            slot = slot + SLOTS.index(landing or name)
        return pltpu.make_async_remote_copy(
            src_ref=part, dst_ref=part, send_sem=send_sem.at[slot], recv_sem=recv_sem.at[slot],
            device_id=target, device_id_type=MESH,
        )

    def axis_of(chunk, name):
        lead = LEADS[chunk]
        other = "y" if lead == "x" else "x"
        return {"p1": lead, "p2": other, "a1": "c", "a2": "c"}.get(name, name)

    def wait_for(chunk, mark):
        if mark == "ZM":
            @pl.when(is_mid)
            def _():
                copy(chunk, "zo", to["zo"], "zoE").wait_recv()
                copy(chunk, "zo", to["zo"], "zoM").wait_recv()
        elif mark == "ZP":
            copy(chunk, "zp", to["zp"]).wait_recv()
        elif mark == "ZF":
            @pl.when(jnp.logical_not(is_mid))
            def _():
                copy(chunk, "zf", to["zf"]).wait_recv()
        else:
            copy(chunk, mark, to[axis_of(chunk, mark)]).wait_recv()

    def event(chunk, stage):
        waits, sends = stages(KINDS[chunk], LEADS[chunk])[stage]
        for mark in waits:
            wait_for(chunk, mark)
        for name, _ in sends:
            begin = copy(chunk, name, to[axis_of(chunk, name)]).start
            if name == "zf":
                pl.when(is_mid)(begin)
            else:
                begin()

    def all_sent():
        for chunk in range(len(KINDS)):
            for _, sends in stages(KINDS[chunk], LEADS[chunk]):
                for name, _ in sends:
                    finish = copy(chunk, name, to[axis_of(chunk, name)]).wait_send
                    if name == "zf":
                        pl.when(is_mid)(finish)
                    else:
                        finish()

    cursor = [0]

    def now():
        for item in PLAN[cursor[0]]:
            event(*item)
        cursor[0] += 1

    def steps(count):
        plan = PLAN[cursor[0]:cursor[0] + count]
        cursor[0] += count

        def run(step):
            for place, items in enumerate(plan):
                if items:
                    @pl.when(step == place)
                    def _():
                        for item in items:
                            event(*item)
        return run

    mine = weights.at[y, x, core, z]
    own = []
    row = 0
    for half in range(HALVES):
        for kind in range(3):
            own.append((qkv_in.at[kind, :, pl.ds(half * WIDE, WIDE)], row, qkv_in.shape[1]))
            row += qkv_in.shape[1]
    own.append((out_in, row, out_in.shape[0]))
    row += out_in.shape[0]
    part = ffn_in.shape[1] // FF_PARTS
    for index in range(FF_PARTS):
        for source in (ffn_in.at[0], ffn_in.at[1], down_in):
            own.append((source.at[pl.ds(index * part, part)], row, part))
            row += part
    loads = [
        pltpu.make_async_copy(source, mine.at[pl.ds(at, rows)], local_sem.at[place])
        for place, (source, at, rows) in enumerate(own)
    ]
    token_load = pltpu.make_async_copy(tokens_in, tokens, token_sem)
    for load in loads:
        load.start()
    token_load.start()
    barrier = pltpu.get_barrier_semaphore()
    for peer in ("x", "y", "c", "zp", "zo", "far"):
        pl.semaphore_signal(barrier, inc=1, device_id=to[peer], device_id_type=MESH)
    pl.semaphore_wait(barrier, 6)
    for load in loads:
        load.wait()
    now()

    total_rows, width = tokens.shape
    blocks = total_rows // ROWS

    def norm_rows(source, gain_row):
        gain = gain_ref[gain_row:gain_row + 1, :]

        def body(step, carry):
            rows = pl.ds(pl.multiple_of(step * 128, 128), 128)
            wide = source[rows, :].astype(jnp.float32)
            square = jnp.mean(wide * wide, axis=-1, keepdims=True)
            normed[rows, :] = (wide * lax.rsqrt(square + 1e-05) * gain).astype(jnp.bfloat16)
            return carry
        lax.fori_loop(0, total_rows // 128, body, 0)

    token_load.wait()
    now()
    norm_rows(tokens, 0)
    now()
    lane = lax.broadcasted_iota(jnp.int32, (1, WIDE), 1)
    half_head = HEAD_DIM // 2
    times = jnp.broadcast_to(time_ref[...].astype(jnp.float32), (WIDE, total_rows)).T
    freq = jnp.exp(lax.rem(lane, half_head).astype(jnp.float32) * (-math.log(10000.0) / half_head))
    front = lax.rem(lane, HEAD_DIM) < half_head
    angle = times * freq
    cosine[...] = jnp.cos(angle)
    sine[...] = jnp.where(front, -1.0, 1.0) * jnp.sin(angle)
    variates = jnp.broadcast_to(variate_ref[...].astype(jnp.float32), (WIDE, total_rows)).T
    spare = lax.rem(lane, HEAD_DIM)
    number = lax.rem(spare, 16).astype(jnp.float32)
    third = spare // 16
    kinds[...] = jnp.where(
        jnp.logical_and(variates == number, third < 3), 1.0, 0.0
    ).astype(jnp.bfloat16)
    samples = sample_ref[...].astype(jnp.float32)
    for quarter in range(total_rows // WIDE):
        rows = slice(quarter * WIDE, (quarter + 1) * WIDE)
        column = jnp.broadcast_to(samples[:, rows], (WIDE, WIDE)).T
        for piece in range(L // WIDE):
            base = quarter * WIDE // L * L + piece * WIDE
            other = samples[:, base:base + WIDE]
            mask[rows, piece * WIDE:(piece + 1) * WIDE] = jnp.where(column == other, 0.0, -1e30)

    left = lane < HEAD_DIM

    def rows_of(at, count, index):
        return jnp.concatenate(
            [
                weights[a, b, c, index, pl.ds(at, count), :]
                for a in range(2) for b in range(2) for c in range(2)
            ],
            axis=0,
        )

    def rotated(raw, factor):
        swapped = jnp.where(
            front, pltpu.roll(raw, WIDE - half_head, 1), pltpu.roll(raw, half_head, 1)
        )
        return ((raw * cosine[...] + swapped * sine[...]) * factor).astype(jnp.bfloat16)

    def project(half, at, kind, held, run, base):
        def body(step, carry):
            run(base + step)
            weight = jnp.concatenate(
                [rows_of(at, width // 8, step * 2), rows_of(at, width // 8, step * 2 + 1)], axis=1
            )
            raw = jnp.dot(normed[...], weight, preferred_element_type=jnp.float32)
            for group in range(2):
                piece = raw[:, group * WIDE:(group + 1) * WIDE]
                if kind == 0:
                    piece = rotated(piece, HEAD_DIM ** -0.5 * LOG2E)
                elif kind == 1:
                    piece = rotated(piece, 1.0)
                else:
                    piece = piece.astype(jnp.bfloat16)
                held[(step * 2 + group) * HALVES + half] = piece
            return carry
        lax.fori_loop(0, 2, body, 0)

    def attend(half, run):
        def body(step, carry):
            run(step)
            pair = step // blocks * HALVES + half
            block = lax.rem(step, blocks)
            rows = pl.ds(pl.multiple_of(block * ROWS, ROWS), ROWS)
            span = pl.ds(pl.multiple_of((block * ROWS) // L * L, L), L)
            both = queries[pair, rows, :]
            key_rows = keys[pair, span, :]
            value_rows = values[pair, span, :]
            own_kinds = kinds[rows, :]
            other_kinds = kinds[span, :]
            one = jnp.ones((), jnp.bfloat16)
            mixed = []
            for side in range(2):
                head = pair * 2 + side
                chosen = left if side == 0 else jnp.logical_not(left)
                gap = jnp.full((1, WIDE), (bias_ref[0, head] - bias_ref[1, head]) * LOG2E, jnp.float32)
                first = gap.astype(jnp.bfloat16).astype(jnp.float32)
                second = (gap - first).astype(jnp.bfloat16).astype(jnp.float32)
                parts = jnp.where(third == 0, first, jnp.where(third == 1, second, gap - first - second))
                query = jnp.where(chosen, both, own_kinds * parts.astype(jnp.bfloat16))
                key = jnp.where(chosen, key_rows, other_kinds)
                value = jnp.where(chosen, value_rows, one)
                scores = lax.dot_general(
                    query, key, (((1,), (1,)), ((), ())), preferred_element_type=jnp.float32
                )
                scores = scores + mask[rows, :]
                top = jnp.max(scores, axis=1, keepdims=True)
                expo = jnp.exp2(scores - top).astype(jnp.bfloat16)
                mixed.append(jnp.dot(expo, value, preferred_element_type=jnp.float32))
            amount = jnp.where(left, mixed[0], mixed[1])
            share = pltpu.roll(jnp.where(left, mixed[1], mixed[0]), HEAD_DIM, 1)
            lanes = pl.ds(pl.multiple_of(pair * WIDE, WIDE), WIDE)
            attended[rows, lanes] = (amount / share).astype(jnp.bfloat16)
            return carry
        lax.fori_loop(0, width // WIDE // HALVES * blocks, body, 0)

    for half in range(HALVES):
        run = steps(6)
        for kind, held in enumerate((queries, keys, values)):
            project(half, spans[half * 3 + kind][0], kind, held, run, kind * 2)
        attend(half, steps(width // WIDE // HALVES * blocks))

    def columns_of(at, count, side_y, side_x):
        return jnp.concatenate(
            [
                jnp.concatenate(
                    [weights[side_y, side_x, c, index, pl.ds(at, count), :] for c in range(2)], axis=1
                )
                for index in range(LAYOUT[1])
            ],
            axis=0,
        )

    slab = 2 * WIDE
    out_at = spans[HALVES * 3][0]
    out_events = steps(4)

    def out_step(step, carry):
        out_events(step)
        lanes = pl.ds(pl.multiple_of(step * slab, slab), slab)
        weight = columns_of(out_at, width // LAYOUT[1], step // 2, lax.rem(step, 2))
        mixed = jnp.dot(attended[...], weight, preferred_element_type=jnp.float32)
        wide = (tokens[:, lanes].astype(jnp.float32) + mixed).astype(jnp.bfloat16)
        residual[:, lanes] = wide
        total[:, lanes] = wide.astype(jnp.float32)
        return carry
    lax.fori_loop(0, 4, out_step, 0)
    now()
    norm_rows(residual, 1)

    def hidden_weight(at):
        return jnp.concatenate(
            [
                jnp.concatenate(
                    [
                        weights[a, b, c, index, pl.ds(at, part), :]
                        for a in range(2) for b in range(2) for c in range(2)
                    ],
                    axis=1,
                )
                for index in range(LAYOUT[1])
            ],
            axis=0,
        )

    def against(at):
        return lax.dot_general(
            normed[...], hidden_weight(at), (((1,), (1,)), ((), ())),
            preferred_element_type=jnp.float32,
        )

    ff_at = spans[HALVES * 3 + 2][0]
    ff_events = steps(FF_PARTS * 4)

    def ff_step(index, carry):
        at = ff_at + index * (3 * part)
        at = pl.multiple_of(at, 16)
        ff_events(index * 4)
        gate[...] = against(at)
        ff_events(index * 4 + 1)
        up = against(pl.multiple_of(at + part, 16))
        opened = gate[...]
        hidden[...] = (opened / (1.0 + jnp.exp(-opened)) * up).astype(jnp.bfloat16)
        for pair in range(2):
            ff_events(index * 4 + 2 + pair)
            for side in range(2):
                lanes = slice((pair * 2 + side) * slab, (pair * 2 + side + 1) * slab)
                weight = columns_of(pl.multiple_of(at + 2 * part, 16), part, pair, side)
                fresh = total[:, lanes] + jnp.dot(
                    hidden[...], weight, preferred_element_type=jnp.float32
                )
                total[:, lanes] = fresh
        return carry
    lax.fori_loop(0, FF_PARTS, ff_step, 0)
    for piece in range(4):
        lanes = slice(piece * slab, (piece + 1) * slab)
        result[:, lanes] = total[:, lanes].astype(jnp.bfloat16)
    save = pltpu.make_async_copy(result, final_ref, result_sem)
    save.start()
    all_sent()
    save.wait()


def spans_of(qkv, out, ffn):
    found, row = [], 0
    for rows in [qkv.shape[1]] * (3 * HALVES) + [out.shape[0] // 2] * 2 + [ffn.shape[1] // FF_PARTS] * (3 * FF_PARTS):
        found.append((row, rows))
        row += rows
    return tuple(found), row


def fused(
    tokens, norm_gain, qkv_weight, out_weight, variate_bias, ffn_weight, down_weight,
    sample_ids, variate_ids, time_ids,
):
    rows, width = tokens.shape
    ffn = jnp.swapaxes(ffn_weight, 1, 2)
    spans, depth = spans_of(qkv_weight, out_weight, ffn)
    vmem = pl.BlockSpec(memory_space=pltpu.VMEM)
    anywhere = pl.BlockSpec(memory_space=pl.ANY)
    per_pair = pltpu.VMEM((width // WIDE, rows, WIDE), jnp.bfloat16)
    flat = pltpu.VMEM((rows, width), jnp.bfloat16)
    strip = pltpu.VMEM((rows, WIDE), jnp.float32)
    ff_wide = LAYOUT[1] * ffn.shape[1] // FF_PARTS
    copies = len(KINDS) * len(SLOTS)
    return pl.pallas_call(
        functools.partial(layer_kernel, spans),
        out_shape=jax.ShapeDtypeStruct((rows, width), jnp.bfloat16),
        in_specs=[pl.BlockSpec(memory_space=pltpu.SMEM)] + [vmem] * 4 + [anywhere] * 5,
        out_specs=anywhere,
        scratch_shapes=[
            pltpu.VMEM((2, 2, 2, LAYOUT[1], depth, WIDE), jnp.bfloat16),
            flat, flat, per_pair, per_pair, per_pair, flat, flat,
            pltpu.VMEM((rows, ff_wide), jnp.float32),
            pltpu.VMEM((rows, ff_wide), jnp.bfloat16),
            pltpu.VMEM((rows, width), jnp.float32),
            strip, strip, pltpu.VMEM((rows, WIDE), jnp.bfloat16),
            pltpu.VMEM((rows, L), jnp.float32),
            flat,
            pltpu.SemaphoreType.DMA((copies,)),
            pltpu.SemaphoreType.DMA((copies,)),
            pltpu.SemaphoreType.DMA((3 * HALVES + 1 + 3 * FF_PARTS,)),
            pltpu.SemaphoreType.DMA(()),
            pltpu.SemaphoreType.DMA(()),
        ],
        compiler_params=pltpu.CompilerParams(
            collective_id=0, has_side_effects=True, vmem_limit_bytes=60 * 1024 * 1024
        ),
    )(
        variate_bias, norm_gain, sample_ids.reshape(1, -1), variate_ids.reshape(1, -1),
        time_ids.reshape(1, -1), tokens, qkv_weight, out_weight, ffn, down_weight,
    )


def solution(mesh):
    body = fused if (mesh.shape["dp"], mesh.shape["mp"]) == LAYOUT else local
    return jax.shard_map(
        body,
        mesh=mesh,
        in_specs=(
            P(("dp", "mp"), None),
            P(),
            P(None, "dp", "mp"),
            P("mp", "dp"),
            P(),
            P(None, "dp", "mp"),
            P("mp", "dp"),
            P(("dp", "mp")),
            P(("dp", "mp")),
            P(("dp", "mp")),
        ),
        out_specs=P(("dp", "mp"), None),
        check_vma=False,
    )
```

time: 135 us -> 109 us (0.81)
  Pallas kernels: 129 us -> 106 us
  local copies, waits for them, and re-layouts: 4.87 us -> 2.26 us
    pallas_call x1, Pallas kernels: 129 us -> 106 us  [fused(): pl.pallas_call(functools.partial(layer_kernel, spans), out_shape=jax.Shap...]
    unnamed x8 -> x1, local copies, waits for them, and re-layouts: 4.87 us -> 2.26 us
where the time goes in v1:
time: 109 us
  Pallas kernels  106 us (97%)
  local copies, waits for them, and re-layouts  2.26 us (2%)
    pallas_call x1, Pallas kernels, fused(): pl.pallas_call(functools.partial(layer_kernel, spans), out_shape=jax.Shap...  106 us
    unnamed x1, local copies, waits for them, and re-layouts  2.26 us

profile of v1, /device:TPU:1, one launch (start us, length us, event | category | flops | bytes accessed | tf_op | source)
XLA Modules:
  0.0 108.6 jit_solution(13309743454467670569)
XLA Ops:
  0.0 106.3 %shard_map.100 = bf16[512,1024]{1,0:T(8,128)(2,1)} custom-call(f32[2,16]{1,0:T(2,128)} %bias_ref.1, f32[2,1024]{1,0:T(2,128)} %gain_ref.1, s32[1,512]{1,0:T(1,128)} %bitcast.5, s32[1,512]{1,0:T(1,128)} %bitcast.6, s32[1,512]{1,0:T(1,128)} %bitcast.7, bf16[512,1024]{1,0:T(8,128)(2,1)} %tokens_in.1, bf16[3,128,256]{2,1,0:T(8,128)(2,1)} %qkv_in.1, ...), custom_call_target="tpu_custom_call" | custom-call | tf_op jit(solution)/shard_map/pallas_call | solution.py:589
  106.4 2.3 %copy.12 = bf16[512,1024]{1,0:T(8,128)(2,1)} copy(bf16[512,1024]{1,0:T(8,128)(2,1)} %shard_map.100) | data formatting | bytes 2097152

commit v2 on v1

--- a/solution.py
+++ b/solution.py
@@ -123,65 +123,57 @@
 
 MESH = pl.DeviceIdType.MESH
 WIDE = 2 * HEAD_DIM
-ROWS = 256
+ROWS = 512
 LAYOUT = (2 ** 3, 2 ** 2)
 HALVES = 2
 FF_PARTS = 4
 LOG2E = math.log2(math.e)
 SLOTS = ("zp", "zoE", "zoM", "zf", "p1", "p2", "a1", "a2")
-KINDS = "AAAAAAABBAAAAAAABBAA"
-LEADS = "xyxyxyxxyyxyxyxyxyxy"
+KINDS = "AAAAAAAAAAABABABABAA"
+LEADS = "xyxyxxyyyxxxyyxxyyxy"
 PLAN = (
-    ((0, 0), (1, 0), (16, 0), (7, 0), (8, 0), (4, 0), (3, 0), (2, 0),),
-    (),
-    (),
-    ((0, 1), (16, 1), (1, 1), (7, 1), (8, 1), (17, 0), (0, 2), (1, 2), (4, 1), (3, 1), (2, 1), (5, 0), (6, 0), (4, 2), (10, 0), (3, 2), (2, 2), (17, 1), (11, 0), (9, 0), (13, 0), (0, 3), (1, 3), (5, 1), (12, 0), (14, 0), (6, 1), (10, 1), (4, 3), (3, 3), (15, 0), (5, 2), (2, 3), (6, 2), (11, 1), (9, 1), (10, 2), (13, 1), (18, 0), (19, 0), (0, 4), (11, 2), (12, 1), (14, 1), (1, 4), (9, 2), (0, 5),),
-    (),
-    ((13, 2), (1, 5), (16, 2), (15, 1), (7, 2),),
-    (),
-    ((12, 2), (14, 2), (4, 4), (3, 4), (5, 3), (8, 2), (2, 4), (6, 3), (4, 5), (3, 5), (18, 1), (19, 1), (2, 5), (10, 3),),
-    (),
-    (),
-    ((15, 2),),
-    ((11, 3),),
-    (),
-    (),
-    (),
-    (),
-    (),
-    (),
-    (),
-    (),
-    (),
-    ((18, 2), (16, 3), (19, 2), (9, 3), (7, 3), (13, 3), (8, 3), (17, 2), (12, 3), (14, 3), (5, 4), (6, 4), (5, 5),),
-    (),
-    (),
-    (),
-    (),
-    (),
-    (),
-    ((15, 3), (10, 4), (6, 5), (16, 4),),
-    (),
-    ((7, 4),),
-    ((10, 5), (16, 5), (7, 5), (18, 3), (19, 3), (11, 4),),
-    (),
-    (),
-    (),
-    (),
-    ((8, 4), (9, 4), (13, 4), (17, 3), (11, 5), (8, 5),),
-    ((9, 5),),
-    ((13, 5), (12, 4),),
-    (),
-    (),
-    ((14, 4), (12, 5),),
-    (),
-    ((14, 5), (15, 4),),
-    (),
-    ((15, 5), (17, 4),),
-    (),
-    (),
-    ((18, 4), (17, 5),),
-    ((19, 4), (18, 5),),
+    ((1, 0), (13, 0), (0, 0), (11, 0), (3, 0), (2, 0), (7, 0), (17, 0), (5, 0), (15, 0),),
+    (),
+    (),
+    ((1, 1), (11, 1), (15, 1), (17, 1), (0, 1), (13, 1), (3, 1), (1, 2), (2, 1), (0, 2), (7, 1), (6, 0), (3, 2), (9, 0), (5, 1), (10, 0), (4, 0), (2, 2), (7, 2), (12, 0), (8, 0), (6, 1), (16, 0), (1, 3), (0, 3), (5, 2), (4, 1), (12, 1), (6, 2), (19, 0), (3, 3), (4, 2), (18, 0), (14, 0), (8, 1), (2, 3), (8, 2), (10, 1), (9, 1), (0, 4), (3, 4), (16, 1), (7, 3), (14, 1), (12, 2), (13, 2), (6, 3), (18, 1), (5, 3), (9, 2), (14, 2), (16, 2), (11, 2), (15, 2), (10, 2), (19, 1), (4, 3), (8, 3), (7, 4), (6, 4), (2, 4), (1, 4), (2, 5), (1, 5), (6, 5), (18, 2), (0, 5),),
+    ((9, 3), (13, 3), (5, 4),),
+    (),
+    (),
+    (),
+    (),
+    (),
+    ((19, 2),),
+    (),
+    ((4, 4), (12, 3), (10, 3), (11, 3),),
+    ((13, 4), (15, 3), (14, 3), (5, 5), (17, 2), (3, 5),),
+    (),
+    ((13, 5), (4, 5),),
+    (),
+    (),
+    (),
+    ((8, 4), (7, 5), (16, 3), (9, 4),),
+    (),
+    (),
+    ((18, 3), (8, 5),),
+    (),
+    (),
+    (),
+    (),
+    (),
+    (),
+    ((10, 4), (12, 4), (11, 4), (19, 3), (10, 5), (9, 5), (17, 3),),
+    (),
+    (),
+    ((11, 5), (15, 4),),
+    ((14, 4), (16, 4), (12, 5),),
+    (),
+    ((14, 5), (15, 5),),
+    (),
+    (),
+    ((17, 4), (16, 5),),
+    (),
+    ((18, 4), (19, 4), (17, 5),),
+    ((18, 5),),
     ((19, 5),),
     (),
 )
@@ -213,7 +205,7 @@
     bias_ref, gain_ref, sample_ref, variate_ref, time_ref, tokens_in, qkv_in, out_in, ffn_in, down_in,
     final_ref,
     weights, tokens, normed, queries, keys, values, attended, residual, gate, hidden, total,
-    cosine, sine, kinds, mask, result, send_sem, recv_sem, local_sem, token_sem, result_sem,
+    cosine, sine, kinds, mask, send_sem, recv_sem, local_sem, token_sem,
 ):
     dp = lax.axis_index("dp")
     z = lax.axis_index("mp")
@@ -557,11 +549,8 @@
     lax.fori_loop(0, FF_PARTS, ff_step, 0)
     for piece in range(4):
         lanes = slice(piece * slab, (piece + 1) * slab)
-        result[:, lanes] = total[:, lanes].astype(jnp.bfloat16)
-    save = pltpu.make_async_copy(result, final_ref, result_sem)
-    save.start()
+        final_ref[:, lanes] = total[:, lanes].astype(jnp.bfloat16)
     all_sent()
-    save.wait()
 
 
 def spans_of(qkv, out, ffn):
@@ -588,9 +577,9 @@
     copies = len(KINDS) * len(SLOTS)
     return pl.pallas_call(
         functools.partial(layer_kernel, spans),
-        out_shape=jax.ShapeDtypeStruct((rows, width), jnp.bfloat16),
+        out_shape=pltpu.VMEM((rows, width), jnp.bfloat16),
         in_specs=[pl.BlockSpec(memory_space=pltpu.SMEM)] + [vmem] * 4 + [anywhere] * 5,
-        out_specs=anywhere,
+        out_specs=pl.BlockSpec(memory_space=pltpu.VMEM),
         scratch_shapes=[
             pltpu.VMEM((2, 2, 2, LAYOUT[1], depth, WIDE), jnp.bfloat16),
             flat, flat, per_pair, per_pair, per_pair, flat, flat,
@@ -599,15 +588,13 @@
             pltpu.VMEM((rows, width), jnp.float32),
             strip, strip, pltpu.VMEM((rows, WIDE), jnp.bfloat16),
             pltpu.VMEM((rows, L), jnp.float32),
-            flat,
             pltpu.SemaphoreType.DMA((copies,)),
             pltpu.SemaphoreType.DMA((copies,)),
             pltpu.SemaphoreType.DMA((3 * HALVES + 1 + 3 * FF_PARTS,)),
             pltpu.SemaphoreType.DMA(()),
-            pltpu.SemaphoreType.DMA(()),
         ],
         compiler_params=pltpu.CompilerParams(
-            collective_id=0, has_side_effects=True, vmem_limit_bytes=60 * 1024 * 1024
+            collective_id=0, has_side_effects=True, vmem_limit_bytes=62 * 1024 * 1024
         ),
     )(
         variate_bias, norm_gain, sample_ids.reshape(1, -1), variate_ids.reshape(1, -1),

time: 109 us -> 106 us (0.972)
  local copies, waits for them, and re-layouts: 2.26 us -> 0.97 us
    pallas_call x1, Pallas kernels: 106 us -> 105 us  [fused(): pl.pallas_call(functools.partial(layer_kernel, spans), out_shape=pltpu.VM...]
    unnamed x1, local copies, waits for them, and re-layouts: 2.26 us -> 0.97 us
where the time goes in v2:
time: 106 us
  Pallas kernels  105 us (99%)
    pallas_call x1, Pallas kernels, fused(): pl.pallas_call(functools.partial(layer_kernel, spans), out_shape=pltpu.VM...  105 us

profile of v2, /device:TPU:1, one launch (start us, length us, event | category | flops | bytes accessed | tf_op | source)
XLA Modules:
  0.0 106.0 jit_solution(14729400841118072346)
XLA Ops:
  0.0 105.0 %shard_map.100 = bf16[512,1024]{1,0:T(8,128)(2,1)S(1)} custom-call(f32[2,16]{1,0:T(2,128)} %bias_ref.1, f32[2,1024]{1,0:T(2,128)} %gain_ref.1, s32[1,512]{1,0:T(1,128)} %bitcast.5, s32[1,512]{1,0:T(1,128)} %bitcast.6, s32[1,512]{1,0:T(1,128)} %bitcast.7, bf16[512,1024]{1,0:T(8,128)(2,1)} %tokens_in.1, bf16[3,128,256]{2,1,0:T(8,128)(2,1)} %qkv_in.1, ...), custom_call_target="tpu_custom_call" | custom-call | tf_op jit(solution)/shard_map/pallas_call | solution.py:578
  105.0 1.0 copy.12

commit v3 on v2

--- a/solution.py
+++ b/solution.py
@@ -133,9 +133,9 @@
 LEADS = "xyxyxxyyyxxxyyxxyyxy"
 PLAN = (
     ((1, 0), (13, 0), (0, 0), (11, 0), (3, 0), (2, 0), (7, 0), (17, 0), (5, 0), (15, 0),),
-    (),
-    (),
-    ((1, 1), (11, 1), (15, 1), (17, 1), (0, 1), (13, 1), (3, 1), (1, 2), (2, 1), (0, 2), (7, 1), (6, 0), (3, 2), (9, 0), (5, 1), (10, 0), (4, 0), (2, 2), (7, 2), (12, 0), (8, 0), (6, 1), (16, 0), (1, 3), (0, 3), (5, 2), (4, 1), (12, 1), (6, 2), (19, 0), (3, 3), (4, 2), (18, 0), (14, 0), (8, 1), (2, 3), (8, 2), (10, 1), (9, 1), (0, 4), (3, 4), (16, 1), (7, 3), (14, 1), (12, 2), (13, 2), (6, 3), (18, 1), (5, 3), (9, 2), (14, 2), (16, 2), (11, 2), (15, 2), (10, 2), (19, 1), (4, 3), (8, 3), (7, 4), (6, 4), (2, 4), (1, 4), (2, 5), (1, 5), (6, 5), (18, 2), (0, 5),),
+    ((1, 1), (11, 1), (15, 1), (17, 1), (0, 1), (13, 1), (3, 1), (1, 2), (2, 1), (0, 2), (7, 1), (6, 0), (3, 2), (9, 0),),
+    ((5, 1), (10, 0), (4, 0), (2, 2), (7, 2), (12, 0), (8, 0), (6, 1), (16, 0), (1, 3),),
+    ((0, 3), (5, 2), (4, 1), (12, 1), (6, 2), (19, 0), (3, 3), (4, 2), (18, 0), (14, 0), (8, 1), (2, 3), (8, 2), (10, 1), (9, 1), (0, 4), (3, 4), (16, 1), (7, 3), (14, 1), (12, 2), (13, 2), (6, 3), (18, 1), (5, 3), (9, 2), (14, 2), (16, 2), (11, 2), (15, 2), (10, 2), (19, 1), (4, 3), (8, 3), (7, 4), (6, 4), (2, 4), (1, 4), (2, 5), (1, 5), (6, 5), (18, 2), (0, 5),),
     ((9, 3), (13, 3), (5, 4),),
     (),
     (),
@@ -202,10 +202,11 @@
 
 def layer_kernel(
     spans,
-    bias_ref, gain_ref, sample_ref, variate_ref, time_ref, tokens_in, qkv_in, out_in, ffn_in, down_in,
+    bias_ref, gain_in, sample_in, variate_in, time_in, tokens_in, qkv_in, out_in, ffn_in, down_in,
     final_ref,
     weights, tokens, normed, queries, keys, values, attended, residual, gate, hidden, total,
-    cosine, sine, kinds, mask, send_sem, recv_sem, local_sem, token_sem,
+    cosine, sine, kinds, mask, gain_ref, sample_ref, variate_ref, time_ref,
+    send_sem, recv_sem, local_sem, input_sem,
 ):
     dp = lax.axis_index("dp")
     z = lax.axis_index("mp")
@@ -341,14 +342,23 @@
         pltpu.make_async_copy(source, mine.at[pl.ds(at, rows)], local_sem.at[place])
         for place, (source, at, rows) in enumerate(own)
     ]
-    token_load = pltpu.make_async_copy(tokens_in, tokens, token_sem)
+    inputs = [
+        pltpu.make_async_copy(source, held, input_sem.at[place])
+        for place, (source, held) in enumerate(
+            (
+                (tokens_in, tokens), (gain_in, gain_ref), (sample_in, sample_ref),
+                (variate_in, variate_ref), (time_in, time_ref),
+            )
+        )
+    ]
     for load in loads:
         load.start()
-    token_load.start()
     barrier = pltpu.get_barrier_semaphore()
     for peer in ("x", "y", "c", "zp", "zo", "far"):
         pl.semaphore_signal(barrier, inc=1, device_id=to[peer], device_id_type=MESH)
     pl.semaphore_wait(barrier, 6)
+    for load in inputs:
+        load.start()
     for load in loads:
         load.wait()
     now()
@@ -367,7 +377,8 @@
             return carry
         lax.fori_loop(0, total_rows // 128, body, 0)
 
-    token_load.wait()
+    for load in inputs:
+        load.wait()
     now()
     norm_rows(tokens, 0)
     now()
@@ -545,11 +556,9 @@
                     hidden[...], weight, preferred_element_type=jnp.float32
                 )
                 total[:, lanes] = fresh
+                final_ref[:, lanes] = fresh.astype(jnp.bfloat16)
         return carry
     lax.fori_loop(0, FF_PARTS, ff_step, 0)
-    for piece in range(4):
-        lanes = slice(piece * slab, (piece + 1) * slab)
-        final_ref[:, lanes] = total[:, lanes].astype(jnp.bfloat16)
     all_sent()
 
 
@@ -568,7 +577,6 @@
     rows, width = tokens.shape
     ffn = jnp.swapaxes(ffn_weight, 1, 2)
     spans, depth = spans_of(qkv_weight, out_weight, ffn)
-    vmem = pl.BlockSpec(memory_space=pltpu.VMEM)
     anywhere = pl.BlockSpec(memory_space=pl.ANY)
     per_pair = pltpu.VMEM((width // WIDE, rows, WIDE), jnp.bfloat16)
     flat = pltpu.VMEM((rows, width), jnp.bfloat16)
@@ -578,7 +586,7 @@
     return pl.pallas_call(
         functools.partial(layer_kernel, spans),
         out_shape=pltpu.VMEM((rows, width), jnp.bfloat16),
-        in_specs=[pl.BlockSpec(memory_space=pltpu.SMEM)] + [vmem] * 4 + [anywhere] * 5,
+        in_specs=[pl.BlockSpec(memory_space=pltpu.SMEM)] + [anywhere] * 9,
         out_specs=pl.BlockSpec(memory_space=pltpu.VMEM),
         scratch_shapes=[
             pltpu.VMEM((2, 2, 2, LAYOUT[1], depth, WIDE), jnp.bfloat16),
@@ -588,10 +596,12 @@
             pltpu.VMEM((rows, width), jnp.float32),
             strip, strip, pltpu.VMEM((rows, WIDE), jnp.bfloat16),
             pltpu.VMEM((rows, L), jnp.float32),
+            pltpu.VMEM(norm_gain.shape, jnp.float32),
+        ] + [pltpu.VMEM((1, rows), jnp.int32)] * 3 + [
             pltpu.SemaphoreType.DMA((copies,)),
             pltpu.SemaphoreType.DMA((copies,)),
             pltpu.SemaphoreType.DMA((3 * HALVES + 1 + 3 * FF_PARTS,)),
-            pltpu.SemaphoreType.DMA(()),
+            pltpu.SemaphoreType.DMA((5,)),
         ],
         compiler_params=pltpu.CompilerParams(
             collective_id=0, has_side_effects=True, vmem_limit_bytes=62 * 1024 * 1024

time: 106 us -> 106 us (level)
  no operation moved by 1% of the time
where the time goes in v3:
time: 106 us
  Pallas kernels  105 us (99%)
    pallas_call x1, Pallas kernels, fused(): pl.pallas_call(functools.partial(layer_kernel, spans), out_shape=pltpu.VM...  105 us

profile of v3, /device:TPU:1, one launch (start us, length us, event | category | flops | bytes accessed | tf_op | source)
XLA Modules:
  0.0 105.8 jit_solution(8985554414215460908)
XLA Ops:
  0.0 104.8 %shard_map.100 = bf16[512,1024]{1,0:T(8,128)(2,1)S(1)} custom-call(f32[2,16]{1,0:T(2,128)} %bias_ref.1, f32[2,1024]{1,0:T(2,128)} %gain_in.1, s32[1,512]{1,0:T(1,128)} %bitcast.5, s32[1,512]{1,0:T(1,128)} %bitcast.6, s32[1,512]{1,0:T(1,128)} %bitcast.7, bf16[512,1024]{1,0:T(8,128)(2,1)} %tokens_in.1, bf16[3,128,256]{2,1,0:T(8,128)(2,1)} %qkv_in.1, ...), custom_call_target="tpu_custom_call" | custom-call | tf_op jit(solution)/shard_map/pallas_call | solution.py:586
  104.8 1.0 copy.12
